TPU v7x, 32 devices: a whole 2x2x4 slice. The times are simulated.
32 devices in a mesh: tower: 8 (over y, x, core), member: 4 (over z).
Axes of the slice: x: 2, y: 2, z: 4, core: 2. Of those that a mesh axis runs over, the one named last changes fastest.
Arguments:
- slabs: bfloat16 [8, 1024, 4096], P('tower', None, 'member'), may hold values from -6 to 6
- cross_down: bfloat16 [8, 2, 4096, 512], P('tower', None, None, 'member'), may hold values from -0.09375 to 0.09375
- cross_up: bfloat16 [8, 2, 4096, 512], P('tower', None, None, 'member'), may hold values from -0.25 to 0.25
- cross_bias: float32 [8, 2, 4096], P('tower'), may hold values from -3 to 3
- projector: bfloat16 [8, 4096, 2048], P('tower'), may hold values from -0.09375 to 0.09375
- placement: int32 [8, 32], P('tower'), may hold values from 0 to 31, each once within a row
- owner: int32 [4, 256], replicated, may hold values from 0 to 255, each once within a row
- inter_grad: bfloat16 [1024, 16384], P(('tower', 'member')), may hold values from -6 to 6
Outputs:
- interactions: float32 [1024, 16384], P(('tower', 'member'))
- slab_grad: bfloat16 [8, 1024, 4096], P('tower', None, 'member')
Inputs may be any that keep to these rules, and one draw needn't show every extreme that they name: Each row of placement names every feature of its tower once. Each row of owner names every sample of its block once.
All inputs are finite; a program needn't handle non-finite values.
Results may differ from a plain program's by a relative error of at most 0.018.
Values may be sent and summed in bfloat16 or wider, within the bound.
No kernel may reach another device: no remote copies, remote signals or barrier semaphores. Data moves between devices by JAX's collectives and lax.ppermute only.
A program may use at most 128 MiB of HBM per device.

v0:
```python
import jax
import jax.numpy as jnp
from jax import lax
from jax.sharding import PartitionSpec as P


def per_device(slabs, cross_down, cross_up, cross_bias, projector, placement, owner, inter_grad):
    gathered = lax.all_to_all(slabs, "member", split_axis=1, concat_axis=2, tiled=True)
    row_count = gathered.shape[1]
    full_width = gathered.shape[2]
    features = placement.shape[1]
    slot_width = full_width // features
    depth_count = cross_down.shape[1]
    order = placement[0]
    inputs = (
        gathered[0]
        .reshape(row_count, features, slot_width)[:, order]
        .reshape(row_count, full_width)
    )
    inputs_f = inputs.astype(jnp.float32)
    biases = cross_bias[0]
    whole_down, whole_up = (
        lax.all_gather(cross_down, "member", axis=3, tiled=True),
        lax.all_gather(cross_up, "member", axis=3, tiled=True),
    )
    current = inputs
    scales = []
    for depth in range(depth_count):
        hidden = jnp.dot(current, whole_down[0, depth], preferred_element_type=jnp.float32).astype(
            jnp.bfloat16
        )
        scale_now = (
            jnp.dot(hidden, whole_up[0, depth].T, preferred_element_type=jnp.float32)
            + biases[depth]
        )
        scales.append(scale_now)
        current = (inputs_f * scale_now + current.astype(jnp.float32)).astype(jnp.bfloat16)
    vector = jnp.dot(current, projector[0], preferred_element_type=jnp.float32).astype(jnp.bfloat16)
    own_row = lax.dynamic_index_in_dim(owner, lax.axis_index("member"), 0, keepdims=False)
    ordered = vector[own_row]
    owned = lax.all_to_all(ordered[:, None, :], "tower", split_axis=0, concat_axis=1, tiled=True)
    owned_rows = owned.shape[0]
    tower_count = owned.shape[1]
    owned_f = owned.reshape(owned_rows, -1, slot_width).astype(jnp.float32)
    vector_count = owned_f.shape[1]
    table = jnp.einsum("bie,bje->bij", owned_f, owned_f) / slot_width
    interactions = table.reshape(owned_rows, vector_count * vector_count)
    cotangent = inter_grad.astype(jnp.float32).reshape(owned_rows, vector_count, vector_count)
    symmetric = cotangent + jnp.swapaxes(cotangent, 1, 2)
    vec_grad = (jnp.einsum("bij,bje->bie", symmetric, owned_f) / slot_width).astype(jnp.bfloat16)
    vec_grad = vec_grad.reshape(owned_rows, tower_count, -1)
    returned = lax.all_to_all(vec_grad, "tower", split_axis=1, concat_axis=0, tiled=True)
    inverse_own = jnp.argsort(own_row)
    local_grad = returned[:, 0, :][inverse_own]
    gradient = jnp.dot(local_grad, projector[0].T, preferred_element_type=jnp.float32)
    accum = jnp.zeros((row_count, full_width), jnp.float32)
    for depth in reversed(range(depth_count)):
        accum = accum + gradient * scales[depth]
        dscale = (gradient * inputs_f).astype(jnp.bfloat16)
        dhidden = jnp.dot(dscale, whole_up[0, depth], preferred_element_type=jnp.float32).astype(
            jnp.bfloat16
        )
        gradient = gradient + jnp.dot(
            dhidden, whole_down[0, depth].T, preferred_element_type=jnp.float32
        )
    total = (gradient + accum).astype(jnp.bfloat16)
    inverse_place = jnp.argsort(order)
    unplaced = total.reshape(row_count, features, slot_width)[:, inverse_place].reshape(
        1, row_count, full_width
    )
    slab_grad = lax.all_to_all(unplaced, "member", split_axis=2, concat_axis=1, tiled=True)
    return (interactions, slab_grad)


def solution(mesh):
    placed = (
        P("tower", None, "member"),
        P("tower", None, None, "member"),
        P("tower", None, None, "member"),
        P("tower", None, None),
        P("tower", None, None),
        P("tower", None),
        P(),
        P(("tower", "member"), None),
    )
    return jax.shard_map(
        per_device,
        mesh=mesh,
        in_specs=placed,
        out_specs=(P(("tower", "member"), None), P("tower", None, "member")),
        check_vma=False,
    )
```

profile of v0, /device:TPU:2, one launch (start us, length us, event | category | flops | bytes accessed | tf_op | source)
XLA Modules:
  0.0 606.8 jit_solution(234920576451379751)
XLA Ops:
  7.2 0.0 copy-start.2
  7.2 0.0 all-gather.3.cloned.1.call-start
  7.2 0.7 all-gather.3.cloned.1.call-update
  7.9 0.0 all-gather.5.cloned.1.call-start
  8.0 0.7 all-gather.5.cloned.1.call-update
  8.7 0.1 copy-done.2
  8.8 5.2 copy.92
  13.9 0.6 broadcast.88
  14.5 12.8 %reduce = bf16[1024,1024]{1,0:T(8,128)(2,1)S(1)} reduce(bf16[1024,1,1024]{2,1,0:T(2,128)(2,1)} %bitcast.161, bf16[]{:T(256)} %broadcast.88), dimensions={1}, to_apply=%bitcast.157.reduce_sub_computation | reduce | bytes 4194306
  27.3 0.0 copy-start.4
  27.3 0.0 copy-start.3
  27.3 2.8 reshape.136
  30.1 5.3 all-to-all-start
  35.4 0.7 compare_select_fusion
  36.1 0.0 copy-done.4
  36.2 0.0 copy-done.3
  36.2 101.2 %all-to-all-done = bf16[4,2,131072]{2,1,0:T(2,128)(2,1)S(1)} async-done(((bf16[4,2,131072]{2,1,0:T(2,128)(2,1)}), bf16[4,2,131072]{2,1,0:T(2,128)(2,1)S(1)}, u32[]{:S(2)}, u32[]{:S(2)}) %all-to-all-start) | async-done | bytes 2097184 | tf_op jit(solution)/shard_map/all_to_all | solution.py:8
  137.4 3.4 reshape.137
  140.8 3.1 copy.52
  143.9 2.6 copy.41
  146.4 4.1 copy.42
  150.5 2.5 gather_fusion
  153.1 53.1 %all-gather.3.cloned.1.call-done = bf16[1,2,4096,512]{3,2,1,0:T(8,128)(2,1)} async-done(((bf16[1,2,4096,128]{3,2,1,0:T(8,128)(2,1)}), bf16[1,2,4096,512]{3,2,1,0:T(8,128)(2,1)}) %all-gather.3.cloned.1.call-update) | async-done | bytes 8388624 | tf_op jit(solution)/shard_map/all_gather | solution.py:23
  206.2 151.8 %all-gather.5.cloned.1.call-done = bf16[1,2,4096,512]{3,2,1,0:T(8,128)(2,1)} async-done(((bf16[1,2,4096,128]{3,2,1,0:T(8,128)(2,1)}), bf16[1,2,4096,512]{3,2,1,0:T(8,128)(2,1)}) %all-gather.5.cloned.1.call-update) | async-done | bytes 8388624 | tf_op jit(solution)/shard_map/all_gather | solution.py:24
  357.9 7.8 %convolution_add_fusion.3 = f32[256,4096]{1,0:T(8,128)} fusion(bf16[1,2,4096,512]{3,2,1,0:T(8,128)(2,1)} %all-gather.5.cloned.1.call-done, f32[4096]{0:T(1024)S(1)} %bitcast.177, bf16[1,2,4096,512]{3,2,1,0:T(8,128)(2,1)} %all-gather.3.cloned.1.call-done, bf16[32,256,128]{2,1,0:T(8,128)(2,1)S(1)} %gather_fusion), kind=kOutput, calls=%fused_computation.16 | convolution fusion | flops 2148663296 | bytes 14696448 | tf_op jit(solution)/shard_map/dot_general | solution.py:33
  365.7 9.1 %convolution_add_fusion.2 = f32[256,4096]{1,0:T(8,128)} fusion(bf16[1,2,4096,512]{3,2,1,0:T(8,128)(2,1)} %all-gather.5.cloned.1.call-done, f32[4096]{0:T(1024)S(1)} %bitcast.176, bf16[1,2,4096,512]{3,2,1,0:T(8,128)(2,1)} %all-gather.3.cloned.1.call-done, f32[256,4096]{1,0:T(8,128)} %convolution_add_fusion.3, bf16[32,256,128]{2,1,0:T(8,128)(2,1)S(1)} %gather_fusion), kind=kOutput, calls=%fused_computation.15 | convolution fusion | flops 2152857600 | bytes 18890752 | tf_op jit(solution)/shard_map/dot_general | solution.py:33
  374.8 12.7 %fusion.15 = bf16[256,2048]{1,0:T(8,128)(2,1)S(1)} fusion(bf16[1,4096,2048]{2,1,0:T(8,128)(2,1)} %param.12, f32[256,4096]{1,0:T(8,128)} %convolution_add_fusion.2, f32[256,4096]{1,0:T(8,128)} %convolution_add_fusion.3, bf16[32,256,128]{2,1,0:T(8,128)(2,1)S(1)} %gather_fusion), kind=kOutput, calls=%fused_computation.32 | convolution fusion | flops 4303880192 | bytes 28311552 | tf_op jit(solution)/shard_map/dot_general | solution.py:38
  387.5 1.4 gather_fusion.1
  388.9 1.4 reduce.1
  390.3 1.8 reshape.138
  392.1 4.2 all-to-all-start.1
  396.3 1.4 convert_bitcast_fusion
  397.7 0.4 copy.58
  398.1 1.8 copy.46
  399.9 10.3 %all-to-all-done.1 = bf16[8,2,32768]{2,1,0:T(2,128)(2,1)S(1)} async-done(((bf16[8,2,32768]{2,1,0:T(2,128)(2,1)}), bf16[8,2,32768]{2,1,0:T(2,128)(2,1)S(1)}, u32[]{:S(2)}, u32[]{:S(2)}) %all-to-all-start.1) | async-done | bytes 1048608 | tf_op jit(solution)/shard_map/all_to_all | solution.py:41
  410.2 3.4 reshape.139
  413.6 2.2 copy.53
  415.8 1.5 copy.45
  417.4 1.6 reshape.92
  418.9 3.0 multiply_convert_fusion
  421.9 1.5 reshape.96
  423.5 1.5 copy.47
  425.0 5.0 all-to-all-start.2
  430.0 3.2 sort.34
  433.2 1.6 sort.35
  434.8 9.1 %all-to-all-done.2 = bf16[32,8,2048]{2,0,1:T(8,128)(2,1)S(1)} async-done(((bf16[32,8,2048]{2,0,1:T(8,128)(2,1)}), bf16[32,8,2048]{2,0,1:T(8,128)(2,1)S(1)}, u32[]{:S(2)}, u32[]{:S(2)}) %all-to-all-start.2) | async-done | bytes 1048608 | tf_op jit(solution)/shard_map/all_to_all | solution.py:52
  443.9 2.3 gather_fusion.2
  446.2 12.7 %fusion = f32[256,4096]{1,0:T(8,128)} fusion(bf16[256,2048]{1,0:T(8,128)(2,1)} %gather_fusion.2, bf16[1,4096,2048]{2,1,0:T(8,128)(2,1)} %param.12), kind=kOutput, calls=%fused_computation.4 | convolution fusion | flops 4294967296 | bytes 22020096 | tf_op jit(solution)/shard_map/dot_general | solution.py:55
  458.9 0.0 copy-done.1
  458.9 10.2 %convolution_add_fusion.1 = f32[256,4096]{1,0:T(8,128)} fusion(f32[256,4096]{1,0:T(8,128)} %fusion, bf16[1,2,4096,512]{3,2,1,0:T(8,128)(2,1)} %all-gather.3.cloned.1.call-done, bf16[1,2,4096,512]{3,2,1,0:T(8,128)(2,1)} %all-gather.5.cloned.1.call-done, bf16[32,256,128]{2,1,0:T(8,128)(2,1)S(1)} %copy-done.1), kind=kOutput, calls=%fused_computation.14 | convolution fusion | flops 2151809024 | bytes 23068672 | tf_op jit(solution)/shard_map/dot_general | solution.py:63
  469.2 13.5 %fusion.26 = bf16[32,32,8,128]{3,2,1,0:T(8,128)(2,1)} fusion(f32[256,4096]{1,0:T(8,128)} %convolution_add_fusion.1, f32[256,4096]{1,0:T(8,128)} %convolution_add_fusion.3, f32[256,4096]{1,0:T(8,128)} %fusion, f32[256,4096]{1,0:T(8,128)} %convolution_add_fusion.2, bf16[1,2,4096,512]{3,2,1,0:T(8,128)(2,1)} %all-gather.3.cloned.1.call-done, ...), kind=kOutput, calls=%fused_computation.43 | convolution fusion | flops 2157051904 | bytes 33554432 | tf_op jit(solution)/shard_map/dot_general | solution.py:63
  482.7 2.2 copy.90
  484.8 2.1 gather_fusion.3
  487.0 3.3 copy.49
  490.2 25.3 %copy.91 = bf16[1,256,4096]{1,0,2:T(2,128)(2,1)} copy(bf16[1,256,4096]{1,2,0:T(8,128)(2,1)S(1)} %bitcast.166) | data formatting | bytes 4194304 | tf_op jit(solution)/shard_map/reshape | solution.py:68
  515.5 21.6 %reduce.2 = bf16[4096,256]{1,0:T(8,128)(2,1)S(1)} reduce(bf16[4096,1,256]{2,1,0:T(2,128)(2,1)} %bitcast.162, bf16[]{:T(256)} %broadcast.88), dimensions={1}, to_apply=%bitcast.156.reduce_sub_computation | reduce | bytes 4194306
  537.1 2.1 reshape.140
  539.2 3.6 all-to-all-start.3
  542.8 0.8 convolution_multiply_fusion
  543.6 2.5 copy.89
  546.2 45.3 %all-to-all-done.3 = bf16[4,2,131072]{2,1,0:T(2,128)(2,1)S(1)} async-done(((bf16[4,2,131072]{2,1,0:T(2,128)(2,1)}), bf16[4,2,131072]{2,1,0:T(2,128)(2,1)S(1)}, u32[]{:S(2)}, u32[]{:S(2)}) %all-to-all-start.3) | async-done | bytes 2097184 | tf_op jit(solution)/shard_map/all_to_all | solution.py:71
  591.5 3.4 reshape.141
  594.8 2.5 copy.54
  597.3 2.4 copy.51
  (13 shorter events, 0.1 us)
Async XLA Ops:
  7.2 1.6 copy-start.2
  7.2 199.0 %all-gather.3.cloned.1.call-start = ((), (), s32[]{:S(2)}) async-start(), calls=%async_computation.4 | async-start | bytes 10485760 | tf_op jit(solution)/shard_map/all_gather | solution.py:23
  7.9 350.0 %all-gather.5.cloned.1.call-start = ((), (), s32[]{:S(2)}) async-start(), calls=%async_computation.5 | async-start | bytes 10485760 | tf_op jit(solution)/shard_map/all_gather | solution.py:24
  27.3 8.8 %copy-start.4 = (s32[1,32]{1,0:T(1,128)S(1)}, s32[1,32]{1,0:T(1,128)}, u32[]{:S(2)}) copy-start(s32[1,32]{1,0:T(1,128)} %param.13) | copy-start | bytes 388
  27.3 8.9 %copy-start.3 = (f32[1,2,4096]{2,1,0:T(2,128)S(1)}, f32[1,2,4096]{2,1,0:T(2,128)}, u32[]{:S(2)}) copy-start(f32[1,2,4096]{2,1,0:T(2,128)} %param.11) | copy-start | bytes 98308
  30.1 107.3 %all-to-all-start = ((bf16[4,2,131072]{2,1,0:T(2,128)(2,1)}), bf16[4,2,131072]{2,1,0:T(2,128)(2,1)S(1)}, u32[]{:S(2)}, u32[]{:S(2)}) async-start(bf16[4,2,131072]{2,1,0:T(2,128)(2,1)} %reshape.136), calls=%async_computation | async-start | bytes 4194304 | tf_op jit(solution)/shard_map/all_to_all | solution.py:8
  153.1 221.7 %copy-start = (bf16[32,256,128]{2,1,0:T(8,128)(2,1)}, bf16[32,256,128]{2,1,0:T(8,128)(2,1)S(1)}, u32[]{:S(2)}) copy-start(bf16[32,256,128]{2,1,0:T(8,128)(2,1)S(1)} %gather_fusion) | copy-start | bytes 6291460
  392.1 18.1 %all-to-all-start.1 = ((bf16[8,2,32768]{2,1,0:T(2,128)(2,1)}), bf16[8,2,32768]{2,1,0:T(2,128)(2,1)S(1)}, u32[]{:S(2)}, u32[]{:S(2)}) async-start(bf16[8,2,32768]{2,1,0:T(2,128)(2,1)} %reshape.138), calls=%async_computation.1 | async-start | bytes 2097152 | tf_op jit(solution)/shard_map/all_to_all | solution.py:41
  425.0 18.9 %all-to-all-start.2 = ((bf16[32,8,2048]{2,0,1:T(8,128)(2,1)}), bf16[32,8,2048]{2,0,1:T(8,128)(2,1)S(1)}, u32[]{:S(2)}, u32[]{:S(2)}) async-start(bf16[32,8,2048]{2,0,1:T(8,128)(2,1)} %copy.47), calls=%async_computation.2 | async-start | bytes 2097152 | tf_op jit(solution)/shard_map/all_to_all | solution.py:52
  446.2 12.7 %copy-start.1 = (bf16[32,256,128]{2,1,0:T(8,128)(2,1)S(1)}, bf16[32,256,128]{2,1,0:T(8,128)(2,1)}, u32[]{:S(2)}) copy-start(bf16[32,256,128]{2,1,0:T(8,128)(2,1)} %copy-done) | copy-start | bytes 6291460
  539.2 52.3 %all-to-all-start.3 = ((bf16[4,2,131072]{2,1,0:T(2,128)(2,1)}), bf16[4,2,131072]{2,1,0:T(2,128)(2,1)S(1)}, u32[]{:S(2)}, u32[]{:S(2)}) async-start(bf16[4,2,131072]{2,1,0:T(2,128)(2,1)} %reshape.140), calls=%async_computation.3 | async-start | bytes 4194304 | tf_op jit(solution)/shard_map/all_to_all | solution.py:71
Sparse Core Ops, SparseCore 0:
  9.5 196.5 all-gather.2
  207.7 150.1 all-gather.4
where the time goes:
time: 612 us; the launch traced here: 607 us
  waiting for transfers between devices  372 us (61%)
  local copies, waits for them, and re-layouts  89.4 us (15%)
  matrix products  69.9 us (11%)
  other arithmetic  42.7 us (7%)
  starting transfers between devices  18.2 us (3%)
  between operations  14.5 us (2%)
    all_gather x1, waiting for transfers between devices, per_device(): lax.all_gather(cross_up, 'member', axis=3, tiled=True)  152 us
    all_to_all x1, waiting for transfers between devices, per_device(): lax.all_to_all(slabs, 'member', split_axis=1, concat_axis=2, tiled=True)  101 us
    all_gather x1, waiting for transfers between devices, per_device(): lax.all_gather(cross_down, 'member', axis=3, tiled=True)  53.1 us
    all_to_all x1, waiting for transfers between devices, per_device(): lax.all_to_all(unplaced, 'member', split_axis=2, concat_axis=1, tiled=True)  45.3 us
    unnamed x3, other arithmetic  35.8 us
    unnamed x23, local copies, waits for them, and re-layouts  33.3 us
    reshape x2, local copies, waits for them, and re-layouts, per_device(): total.reshape(row_count, features, slot_width)[:, inverse_place]  27.4 us
    dot_general x2, matrix products, per_device(): jnp.dot(dhidden, whole_down[0, depth].T, preferred_element_type=jnp.float32)  23.7 us
  transfers between devices with their start and end apart: 6, of which 6 were waited for; matrix products, arithmetic and copies ran while one was open for 8% of the time, Pallas kernels for 0%

commit v1 on v0

--- a/solution.py
+++ b/solution.py
@@ -2,6 +2,13 @@
 import jax.numpy as jnp
 from jax import lax
 from jax.sharding import PartitionSpec as P
+
+
+def swap_blocks(x, name, split, join):
+    count = lax.axis_size(name)
+    blocks = jnp.stack(jnp.split(x, count, axis=split), axis=0)
+    blocks = lax.all_to_all(blocks, name, split_axis=0, concat_axis=0)
+    return jnp.concatenate(blocks, axis=join)
 
 
 def per_device(slabs, cross_down, cross_up, cross_bias, projector, placement, owner, inter_grad):
@@ -68,7 +75,7 @@
     unplaced = total.reshape(row_count, features, slot_width)[:, inverse_place].reshape(
         1, row_count, full_width
     )
-    slab_grad = lax.all_to_all(unplaced, "member", split_axis=2, concat_axis=1, tiled=True)
+    slab_grad = swap_blocks(unplaced, "member", 2, 1)
     return (interactions, slab_grad)
 
 

time: 612 us -> 571 us (0.933)
  other arithmetic: 42.7 us -> 21.5 us
  local copies, waits for them, and re-layouts: 89.4 us -> 68.6 us
    reshape x2 -> x1, local copies, waits for them, and re-layouts: 27.4 us -> 2.16 us  [per_device(): total.reshape(row_count, features, slot_width)[:, inverse_place]]
    unnamed x3 -> x2, other arithmetic: 35.8 us -> 12.9 us
    unnamed x23 -> x22, local copies, waits for them, and re-layouts: 33.3 us -> 37.6 us
where the time goes in v1:
time: 571 us; the launch traced here: 566 us
  waiting for transfers between devices  374 us (65%)
  matrix products  69.9 us (12%)
  local copies, waits for them, and re-layouts  68.6 us (12%)
  other arithmetic  21.5 us (4%)
  starting transfers between devices  18.1 us (3%)
  between operations  14.3 us (3%)
    all_gather x1, waiting for transfers between devices, per_device(): lax.all_gather(cross_up, 'member', axis=3, tiled=True)  152 us
    all_to_all x1, waiting for transfers between devices, per_device(): lax.all_to_all(slabs, 'member', split_axis=1, concat_axis=2, tiled=True)  101 us
    all_gather x1, waiting for transfers between devices, per_device(): lax.all_gather(cross_down, 'member', axis=3, tiled=True)  53.1 us
    all_to_all x1, waiting for transfers between devices, swap_blocks(): blocks = lax.all_to_all(blocks, name, split_axis=0, concat_axis=0)  45.3 us
    unnamed x22, local copies, waits for them, and re-layouts  37.6 us
    dot_general x2, matrix products, per_device(): jnp.dot(dhidden, whole_down[0, depth].T, preferred_element_type=jnp.float32)  23.7 us
    dot_general x2, matrix products, per_device(): jnp.dot(hidden, whole_up[0, depth].T, preferred_element_type=jnp.float32)  16.9 us
    unnamed x2, other arithmetic  12.9 us
  transfers between devices with their start and end apart: 6, of which 6 were waited for; matrix products, arithmetic and copies ran while one was open for 8% of the time, Pallas kernels for 0%

profile of v1, /device:TPU:2, one launch (start us, length us, event | category | flops | bytes accessed | tf_op | source)
XLA Modules:
  0.0 565.8 jit_solution(3872242795952572050)
XLA Ops:
  7.2 0.0 copy-start.2
  7.2 0.0 all-gather.3.cloned.1.call-start
  7.2 0.7 all-gather.3.cloned.1.call-update
  7.9 0.0 all-gather.5.cloned.1.call-start
  8.0 0.7 all-gather.5.cloned.1.call-update
  8.7 0.1 copy-done.2
  8.8 5.2 copy.101
  13.9 0.5 broadcast.88
  14.5 12.8 %reduce = bf16[1024,1024]{1,0:T(8,128)(2,1)S(1)} reduce(bf16[1024,1,1024]{2,1,0:T(2,128)(2,1)} %bitcast.162, bf16[]{:T(256)} %broadcast.88), dimensions={1}, to_apply=%bitcast.158.reduce_sub_computation | reduce | bytes 4194306
  27.2 0.0 copy-start.5
  27.2 0.0 copy-start.4
  27.3 2.8 reshape.140
  30.0 5.2 all-to-all-start
  35.2 0.7 compare_select_fusion
  35.9 0.0 copy-done.5
  36.0 0.0 copy-done.4
  36.0 101.4 %all-to-all-done = bf16[4,2,131072]{2,1,0:T(2,128)(2,1)S(1)} async-done(((bf16[4,2,131072]{2,1,0:T(2,128)(2,1)}), bf16[4,2,131072]{2,1,0:T(2,128)(2,1)S(1)}, u32[]{:S(2)}, u32[]{:S(2)}) %all-to-all-start) | async-done | bytes 2097184 | tf_op jit(solution)/shard_map/all_to_all | solution.py:15
  137.4 3.3 reshape.141
  140.8 3.1 copy.64
  143.8 2.6 copy.54
  146.4 4.1 copy.55
  150.5 2.5 gather_fusion
  153.0 0.0 copy-start
  153.1 53.1 %all-gather.3.cloned.1.call-done = bf16[1,2,4096,512]{3,2,1,0:T(8,128)(2,1)} async-done(((bf16[1,2,4096,128]{3,2,1,0:T(8,128)(2,1)}), bf16[1,2,4096,512]{3,2,1,0:T(8,128)(2,1)}) %all-gather.3.cloned.1.call-update) | async-done | bytes 8388624 | tf_op jit(solution)/shard_map/all_gather | solution.py:30
  206.2 151.8 %all-gather.5.cloned.1.call-done = bf16[1,2,4096,512]{3,2,1,0:T(8,128)(2,1)} async-done(((bf16[1,2,4096,128]{3,2,1,0:T(8,128)(2,1)}), bf16[1,2,4096,512]{3,2,1,0:T(8,128)(2,1)}) %all-gather.5.cloned.1.call-update) | async-done | bytes 8388624 | tf_op jit(solution)/shard_map/all_gather | solution.py:31
  357.9 7.8 %convolution_add_fusion.3 = f32[256,4096]{1,0:T(8,128)} fusion(bf16[1,2,4096,512]{3,2,1,0:T(8,128)(2,1)} %all-gather.5.cloned.1.call-done, f32[4096]{0:T(1024)S(1)} %bitcast.175, bf16[1,2,4096,512]{3,2,1,0:T(8,128)(2,1)} %all-gather.3.cloned.1.call-done, bf16[32,256,128]{2,1,0:T(8,128)(2,1)S(1)} %gather_fusion), kind=kOutput, calls=%fused_computation.16 | convolution fusion | flops 2148663296 | bytes 14696448 | tf_op jit(solution)/shard_map/dot_general | solution.py:40
  365.7 9.1 %convolution_add_fusion.2 = f32[256,4096]{1,0:T(8,128)} fusion(bf16[1,2,4096,512]{3,2,1,0:T(8,128)(2,1)} %all-gather.5.cloned.1.call-done, f32[4096]{0:T(1024)S(1)} %bitcast.174, bf16[1,2,4096,512]{3,2,1,0:T(8,128)(2,1)} %all-gather.3.cloned.1.call-done, f32[256,4096]{1,0:T(8,128)} %convolution_add_fusion.3, bf16[32,256,128]{2,1,0:T(8,128)(2,1)S(1)} %gather_fusion), kind=kOutput, calls=%fused_computation.15 | convolution fusion | flops 2152857600 | bytes 18890752 | tf_op jit(solution)/shard_map/dot_general | solution.py:40
  374.8 12.7 %fusion.15 = bf16[256,2048]{1,0:T(8,128)(2,1)S(1)} fusion(bf16[1,4096,2048]{2,1,0:T(8,128)(2,1)} %param.12, f32[256,4096]{1,0:T(8,128)} %convolution_add_fusion.2, f32[256,4096]{1,0:T(8,128)} %convolution_add_fusion.3, bf16[32,256,128]{2,1,0:T(8,128)(2,1)S(1)} %gather_fusion), kind=kOutput, calls=%fused_computation.32 | convolution fusion | flops 4303880192 | bytes 28311552 | tf_op jit(solution)/shard_map/dot_general | solution.py:45
  387.5 1.4 gather_fusion.1
  388.9 0.0 copy-start.3
  388.9 1.5 reduce.1
  390.4 14.1 %reshape.142 = bf16[8,2,32768]{2,1,0:T(2,128)(2,1)} reshape(bf16[256,2048]{1,0:T(8,128)(2,1)S(1)} %reduce.1) | data formatting | bytes 2097152
  404.5 4.2 all-to-all-start.1
  408.7 0.0 copy-done.3
  408.7 0.1 convert_bitcast_fusion
  408.8 0.4 copy.69
  409.2 1.8 copy.59
  411.0 11.5 %all-to-all-done.1 = bf16[8,2,32768]{2,1,0:T(2,128)(2,1)S(1)} async-done(((bf16[8,2,32768]{2,1,0:T(2,128)(2,1)}), bf16[8,2,32768]{2,1,0:T(2,128)(2,1)S(1)}, u32[]{:S(2)}, u32[]{:S(2)}) %all-to-all-start.1) | async-done | bytes 1048608 | tf_op jit(solution)/shard_map/all_to_all | solution.py:48
  422.6 3.4 reshape.143
  426.0 2.2 copy.65
  428.2 1.5 copy.58
  429.7 1.6 reshape.95
  431.3 3.0 multiply_convert_fusion
  434.3 1.5 reshape.99
  435.8 1.5 copy.60
  437.4 5.0 all-to-all-start.2
  442.4 3.2 sort.34
  445.5 1.6 sort.35
  447.2 9.1 %all-to-all-done.2 = bf16[32,8,2048]{2,0,1:T(8,128)(2,1)S(1)} async-done(((bf16[32,8,2048]{2,0,1:T(8,128)(2,1)}), bf16[32,8,2048]{2,0,1:T(8,128)(2,1)S(1)}, u32[]{:S(2)}, u32[]{:S(2)}) %all-to-all-start.2) | async-done | bytes 1048608 | tf_op jit(solution)/shard_map/all_to_all | solution.py:59
  456.3 2.3 gather_fusion.2
  458.6 12.7 %fusion = f32[256,4096]{1,0:T(8,128)} fusion(bf16[256,2048]{1,0:T(8,128)(2,1)} %gather_fusion.2, bf16[1,4096,2048]{2,1,0:T(8,128)(2,1)} %param.12), kind=kOutput, calls=%fused_computation.4 | convolution fusion | flops 4294967296 | bytes 22020096 | tf_op jit(solution)/shard_map/dot_general | solution.py:62
  471.3 0.0 copy-done.1
  471.3 10.2 %convolution_add_fusion.1 = f32[256,4096]{1,0:T(8,128)} fusion(f32[256,4096]{1,0:T(8,128)} %fusion, bf16[1,2,4096,512]{3,2,1,0:T(8,128)(2,1)} %all-gather.3.cloned.1.call-done, bf16[1,2,4096,512]{3,2,1,0:T(8,128)(2,1)} %all-gather.5.cloned.1.call-done, bf16[32,256,128]{2,1,0:T(8,128)(2,1)S(1)} %copy-done.1), kind=kOutput, calls=%fused_computation.14 | convolution fusion | flops 2151809024 | bytes 23068672 | tf_op jit(solution)/shard_map/dot_general | solution.py:70
  481.6 13.5 %fusion.26 = bf16[32,32,8,128]{3,2,1,0:T(8,128)(2,1)} fusion(f32[256,4096]{1,0:T(8,128)} %convolution_add_fusion.1, f32[256,4096]{1,0:T(8,128)} %convolution_add_fusion.3, f32[256,4096]{1,0:T(8,128)} %fusion, f32[256,4096]{1,0:T(8,128)} %convolution_add_fusion.2, bf16[1,2,4096,512]{3,2,1,0:T(8,128)(2,1)} %all-gather.3.cloned.1.call-done, ...), kind=kOutput, calls=%fused_computation.44 | convolution fusion | flops 2157051904 | bytes 33554432 | tf_op jit(solution)/shard_map/dot_general | solution.py:70
  495.0 2.2 copy.100
  497.2 2.1 gather_fusion.3
  499.3 3.3 copy.62
  502.6 0.1 slice_bitcast_fusion.33
  502.7 1.6 pad_maximum_fusion
  504.3 3.6 all-to-all-start.3
  507.9 0.8 convolution_multiply_fusion
  508.8 2.5 copy.99
  511.3 45.3 %all-to-all-done.3 = bf16[4,1,256,1024]{2,3,1,0:T(8,128)(2,1)S(1)} async-done(((bf16[4,1,256,1024]{2,3,1,0:T(8,128)(2,1)}), bf16[4,1,256,1024]{2,3,1,0:T(8,128)(2,1)S(1)}, u32[]{:S(2)}, u32[]{:S(2)}) %all-to-all-start.3) | async-done | bytes 2097184 | tf_op jit(solution)/shard_map/all_to_all | solution.py:10
  556.6 2.4 copy.63
  (12 shorter events, 0.1 us)
Async XLA Ops:
  7.2 1.6 copy-start.2
  7.2 199.0 %all-gather.3.cloned.1.call-start = ((), (), s32[]{:S(2)}) async-start(), calls=%async_computation.4 | async-start | bytes 10485760 | tf_op jit(solution)/shard_map/all_gather | solution.py:30
  7.9 350.0 %all-gather.5.cloned.1.call-start = ((), (), s32[]{:S(2)}) async-start(), calls=%async_computation.5 | async-start | bytes 10485760 | tf_op jit(solution)/shard_map/all_gather | solution.py:31
  27.2 8.7 %copy-start.5 = (s32[1,32]{1,0:T(1,128)S(1)}, s32[1,32]{1,0:T(1,128)}, u32[]{:S(2)}) copy-start(s32[1,32]{1,0:T(1,128)} %param.13) | copy-start | bytes 388
  27.2 8.7 %copy-start.4 = (f32[1,2,4096]{2,1,0:T(2,128)S(1)}, f32[1,2,4096]{2,1,0:T(2,128)}, u32[]{:S(2)}) copy-start(f32[1,2,4096]{2,1,0:T(2,128)} %param.11) | copy-start | bytes 98308
  30.0 107.4 %all-to-all-start = ((bf16[4,2,131072]{2,1,0:T(2,128)(2,1)}), bf16[4,2,131072]{2,1,0:T(2,128)(2,1)S(1)}, u32[]{:S(2)}, u32[]{:S(2)}) async-start(bf16[4,2,131072]{2,1,0:T(2,128)(2,1)} %reshape.140), calls=%async_computation | async-start | bytes 4194304 | tf_op jit(solution)/shard_map/all_to_all | solution.py:15
  153.0 221.7 %copy-start = (bf16[32,256,128]{2,1,0:T(8,128)(2,1)}, bf16[32,256,128]{2,1,0:T(8,128)(2,1)S(1)}, u32[]{:S(2)}) copy-start(bf16[32,256,128]{2,1,0:T(8,128)(2,1)S(1)} %gather_fusion) | copy-start | bytes 6291460
  388.9 19.8 %copy-start.3 = (bf16[32,16384]{1,0:T(8,128)(2,1)S(1)}, bf16[32,16384]{1,0:T(8,128)(2,1)}, u32[]{:S(2)}) copy-start(bf16[32,16384]{1,0:T(8,128)(2,1)} %param.15) | copy-start | bytes 3145732
  404.5 18.1 %all-to-all-start.1 = ((bf16[8,2,32768]{2,1,0:T(2,128)(2,1)}), bf16[8,2,32768]{2,1,0:T(2,128)(2,1)S(1)}, u32[]{:S(2)}, u32[]{:S(2)}) async-start(bf16[8,2,32768]{2,1,0:T(2,128)(2,1)} %reshape.142), calls=%async_computation.1 | async-start | bytes 2097152 | tf_op jit(solution)/shard_map/all_to_all | solution.py:48
  437.4 18.9 %all-to-all-start.2 = ((bf16[32,8,2048]{2,0,1:T(8,128)(2,1)}), bf16[32,8,2048]{2,0,1:T(8,128)(2,1)S(1)}, u32[]{:S(2)}, u32[]{:S(2)}) async-start(bf16[32,8,2048]{2,0,1:T(8,128)(2,1)} %copy.60), calls=%async_computation.2 | async-start | bytes 2097152 | tf_op jit(solution)/shard_map/all_to_all | solution.py:59
  458.6 12.7 %copy-start.1 = (bf16[32,256,128]{2,1,0:T(8,128)(2,1)S(1)}, bf16[32,256,128]{2,1,0:T(8,128)(2,1)}, u32[]{:S(2)}) copy-start(bf16[32,256,128]{2,1,0:T(8,128)(2,1)} %copy-done) | copy-start | bytes 6291460
  504.3 52.3 %all-to-all-start.3 = ((bf16[4,1,256,1024]{2,3,1,0:T(8,128)(2,1)}), bf16[4,1,256,1024]{2,3,1,0:T(8,128)(2,1)S(1)}, u32[]{:S(2)}, u32[]{:S(2)}) async-start(bf16[4,1,256,1024]{2,3,1,0:T(8,128)(2,1)} %pad_maximum_fusion), calls=%async_computation.3 | async-start | bytes 4194304 | tf_op jit(solution)/shard_map/all_to_all | solution.py:10
Sparse Core Ops, SparseCore 0:
  9.5 196.5 all-gather.2
  207.7 150.1 all-gather.4
